TPU v7x, 32 devices: a whole 2x2x4 slice. The times are simulated.
32 devices in a mesh: lat: 4 (over z), lon: 4 (over y, x), fold: 2 (over core).
Axes of the slice: x: 2, y: 2, z: 4, core: 2. Of those that a mesh axis runs over, the one named last changes fastest.
Arguments:
- field: float32 [2, 12, 640, 2560], P('fold', None, 'lat', 'lon'), may hold values from -6 to 6
- row_shift: int32 [2, 12, 640, 2560], P('fold', None, 'lat', 'lon'), may hold values from -4 to 4
- col_shift: int32 [2, 12, 640, 2560], P('fold', None, 'lat', 'lon'), may hold values from -4 to 4
- row_frac: bfloat16 [2, 12, 640, 2560], P('fold', None, 'lat', 'lon'), may hold values from 0 to 1
- col_frac: bfloat16 [2, 12, 640, 2560], P('fold', None, 'lat', 'lon'), may hold values from 0 to 1
- wave_map: int32 [16], replicated, may hold values from 0 to 1279, as said below
- legendre: float32 [16, 640, 1280], P('lon', 'lat'), may hold values from -0.25 to 0.25
- helm_coef: float32 [12], P('fold'), may hold values from 1e-06 to 0.0001
Outputs:
- spectrum: float32 [12, 4, 4, 2560], P('fold', 'lon', 'lat')
Inputs may be any that keep to these rules, and one draw needn't show every extreme that they name: `col_shift`: longitude offset of the departure cell. `wave_map`: distinct zonal wavenumbers.
All inputs are finite; a program needn't handle non-finite values.
Results may differ from a plain program's by a relative error of at most 0.0003.
Values sent between devices are 32-bit elements; how exact they have to be, the bound alone decides.
A program may use at most 64 MiB of HBM per device.

v0:
```python
import functools
import math

import jax
import jax.numpy as jnp
from jax import lax
from jax.experimental import pallas as pl
from jax.experimental.pallas import tpu as pltpu
from jax.sharding import PartitionSpec as P

SHIFT_MAX = 4
LANES = 128
HEAD = 8


def cubic_weights(t):
    tm, tp, td = t - 1.0, t + 1.0, t - 2.0
    outer = t * tm
    inner = tp * td
    return (
        outer * (td * (-1.0 / 6.0)),
        inner * (tm * 0.5),
        inner * (t * -0.5),
        outer * (tp * (1.0 / 6.0)),
    )


def interp_kernel(
    margin,
    last,
    field,
    north,
    below,
    mirror,
    west,
    east,
    row_shift,
    col_shift,
    row_frac,
    col_frac,
    table,
    out,
    padded,
    source,
    row_t,
    col_t,
    grid,
):
    rows, cols = field.shape[1:]
    count = cols // LANES
    span = rows + 2 * HEAD
    row_t[...] = row_frac[0].astype(jnp.float32)
    col_t[...] = col_frac[0].astype(jnp.float32)
    inner = slice(LANES, LANES + cols)
    padded[0:HEAD, inner] = north[0]
    padded[HEAD : HEAD + rows, inner] = field[0]
    at_last = jnp.full((1, cols), last[0], jnp.int32) == 1
    for i in range(HEAD):
        line = jnp.where(at_last, mirror[0, HEAD - 1 - i : HEAD - i], below[0, i : i + 1])
        padded[HEAD + rows + i : HEAD + rows + i + 1, inner] = line
    padded[:, LANES - HEAD : LANES] = west[0].T
    padded[:, LANES + cols : LANES + cols + HEAD] = east[0].T

    lane = lax.broadcasted_iota(jnp.int32, (span, LANES), 1)
    for c in range(2 * margin):
        move = c + 1 - margin
        side = (move > 0) - (move < 0)
        near = [
            padded[:, (t + 1) * LANES : (t + 2) * LANES]
            for t in range(min(0, side), count + max(0, side))
        ]
        if side:
            near = [pltpu.roll(x, -move % LANES, 1) for x in near]
        for t in range(count):
            if side > 0:
                source[c, t] = jnp.where(lane < LANES - move, near[t], near[t + 1])
            elif side < 0:
                source[c, t] = jnp.where(lane >= -move, near[t + 1], near[t])
            else:
                source[c, t] = near[t]

    blocks = rows // 8
    unroll = next(u for u in (2, 1) if blocks % u == 0)
    window = range(1 - margin, margin + 1)

    for t in range(count):

        def read(ref, at):
            return ref[at, t * LANES : (t + 1) * LANES]

        def one(j):
            at = pl.ds(pl.multiple_of(8 * j, 8), 8)
            cs = read(col_shift.at[0], at)
            rs = read(row_shift.at[0], at)
            wc = cubic_weights(read(col_t, at))
            wr = cubic_weights(read(row_t, at))
            lines = [None] * len(window)
            hits = [cs == v for v in range(-SHIFT_MAX, SHIFT_MAX + 1)]
            spread = []
            for place_at in range(len(window)):
                w = None
                for step in range(4):
                    v = place_at - step
                    if 0 <= v < len(hits):
                        w = jnp.where(hits[v], wc[step], 0.0 if w is None else w)
                spread.append(w)
            for slot, offset in enumerate(window):
                for c in range(len(window)):
                    cells = source[c, t, pl.ds(8 * j + (HEAD + offset), 8), :]
                    term = spread[c] * cells
                    lines[slot] = term if c == 0 else lines[slot] + term
            left = rs + SHIFT_MAX
            reach = SHIFT_MAX
            while reach >= 1:
                far = left >= reach + (1 if reach > 1 else 0)
                taps = len(lines) - reach
                lines = [jnp.where(far, lines[i + reach], lines[i]) for i in range(taps)]
                left = jnp.where(far, left - reach, left)
                if reach == 1:
                    break
                reach //= 2
            far = left >= 1
            if len(lines) > 4:
                lines = [jnp.where(far, lines[i + 1], lines[i]) for i in range(4)]
            total = wr[0] * lines[0]
            for step in range(1, 4):
                total = total + wr[step] * lines[step]
            grid[at, t * LANES : (t + 1) * LANES] = total

        def body(outer, carry):
            for k in range(unroll):
                one(outer * unroll + k)
            return carry

        lax.fori_loop(0, blocks // unroll, body, 0)

    half = table.shape[1] // 2
    values = grid[...]
    top = values.astype(jnp.bfloat16)
    rest = (values - top.astype(jnp.float32)).astype(jnp.bfloat16)
    both = jnp.dot(top, table[...], preferred_element_type=jnp.float32)
    more = jnp.dot(rest, table[:, :half], preferred_element_type=jnp.float32)
    sums = both[:, :half] + both[:, half:] + more
    out[0] = sums.T.reshape(out.shape[1:])


def interpolated_waves(field, halos, shifts, fracs, table, last, n_lon, margin):
    levels, rows, cols = field.shape

    def whole(x):
        return pl.BlockSpec((1,) + x.shape[1:], lambda i: (i, 0, 0))

    operands = [field, *halos, *shifts, *fracs]
    shape = (levels, n_lon, table.shape[1] // 2 // n_lon, rows)
    return pl.pallas_call(
        functools.partial(interp_kernel, margin),
        grid=(levels,),
        in_specs=[pl.BlockSpec(memory_space=pltpu.SMEM)]
        + [whole(x) for x in operands]
        + [pl.BlockSpec(table.shape, lambda i: (0, 0))],
        out_specs=pl.BlockSpec((1,) + shape[1:], lambda i: (i, 0, 0, 0)),
        out_shape=jax.ShapeDtypeStruct(shape, jnp.float32),
        scratch_shapes=[
            pltpu.VMEM((rows + 2 * HEAD, cols + 2 * LANES), jnp.float32),
            pltpu.VMEM((2 * margin, cols // LANES, rows + 2 * HEAD, LANES), jnp.float32),
            pltpu.VMEM((rows, cols), jnp.float32),
            pltpu.VMEM((rows, cols), jnp.float32),
            pltpu.VMEM((rows, cols), jnp.float32),
        ],
    )(last, *operands, table)


def zonal_table(waves, first_col, cols, lon_total):
    col = first_col + lax.iota(jnp.int32, cols)
    phase = waves[:, None] * col[None, :] % lon_total
    angle = phase.astype(jnp.float32) * (2.0 * math.pi / lon_total)
    pair = jnp.stack([jnp.cos(angle), -jnp.sin(angle)], axis=1) / math.sqrt(lon_total)
    full = pair.reshape(-1, cols)
    top = full.astype(jnp.bfloat16)
    rest = (full - lax.reduce_precision(full, 8, 7)).astype(jnp.bfloat16)
    return jnp.concatenate([top, rest], axis=0).T


def halos_of(grid):
    rows, cols = grid.shape[1:]
    n_lat, n_fold, n_lon = (lax.axis_size(a) for a in ("lat", "fold", "lon"))
    last = n_lat - 1
    at_last = lax.axis_index("lat") == last
    head, tail = grid[:, :HEAD], grid[:, rows - HEAD :]
    north = lax.ppermute(tail, "lat", [(i, i + 1) for i in range(last)])
    below = lax.ppermute(head, "lat", [(i + 1, i) for i in range(last)])
    route = [(last * n_fold + f, last * n_fold + (f ^ 1)) for f in range(n_fold)]
    mirror = lax.ppermute(tail, ("lat", "fold"), route)

    def edge(a, b):
        south = jnp.where(at_last, mirror[:, ::-1, a:b], below[:, :, a:b])
        strip = jnp.concatenate([north[:, :, a:b], grid[:, :, a:b], south], axis=1)
        return jnp.swapaxes(strip, 1, 2)

    ring = [(i, (i + 1) % n_lon) for i in range(n_lon)]
    west = lax.ppermute(edge(cols - HEAD, cols), "lon", ring)
    east = lax.ppermute(edge(0, HEAD), "lon", [(b, a) for a, b in ring])
    return at_last.astype(jnp.int32).reshape(1), (north, below, mirror, west, east)


def scatter_sum(pieces, axis):
    count = lax.axis_size(axis)
    place = lax.axis_index(axis)
    total = lax.dynamic_index_in_dim(pieces, place, 0, keepdims=False)
    arrived = []
    for step in range(1, count):
        piece = lax.dynamic_index_in_dim(pieces, (place + step) % count, 0, keepdims=False)
        arrived.append(lax.ppermute(piece, axis, [(i, (i + step) % count) for i in range(count)]))
    for part in arrived:
        total = total + part
    return total


def local(field, row_shift, col_shift, row_frac, col_frac, wave_map, legendre, helm_coef):
    margin = SHIFT_MAX + 2
    grid = field[0]
    levels, rows, cols = grid.shape
    half = levels // 2
    n_lon, n_lat, n_fold = (lax.axis_size(a) for a in ("lon", "lat", "fold"))
    lon_place = lax.axis_index("lon")
    table = zonal_table(wave_map, lon_place * cols, cols, cols * n_lon)
    last, halos = halos_of(grid)
    waves_here = interpolated_waves(
        grid,
        halos,
        (row_shift[0], col_shift[0]),
        (row_frac[0], col_frac[0]),
        table,
        last,
        n_lon,
        margin,
    )
    slots_here = wave_map.shape[0] // n_lon
    hemisphere = lax.axis_index("fold") % 2
    sign = (1 - 2 * hemisphere).astype(jnp.float32)
    coeffs = scatter_sum(jnp.swapaxes(waves_here, 0, 1), "lon")
    outgoing = lax.dynamic_slice_in_dim(coeffs, (1 - hemisphere) * half, half, 0)
    incoming = lax.ppermute(outgoing, "fold", [(f, f ^ 1) for f in range(n_fold)])
    kept = lax.dynamic_slice_in_dim(coeffs, hemisphere * half, half, 0)
    folded = jnp.stack([kept + incoming, sign * (kept - incoming)], axis=0)
    folded = jnp.transpose(folded.reshape(2, half, slots_here, 2, rows), (2, 3, 0, 1, 4))
    degree_count = legendre.shape[2]
    degrees = lax.iota(jnp.int32, degree_count)
    waves = lax.dynamic_slice_in_dim(wave_map, lon_place * slots_here, slots_here)
    product = jnp.einsum("sqelk,skn->selqn", folded, legendre, precision=lax.Precision.HIGHEST)
    parity = (waves[:, None] + degrees[None, :]) % 2 == 0
    keep = degrees[None, :] >= waves[:, None]
    picked = jnp.where(parity[:, None, None, :], product[:, 0], product[:, 1])
    picked = jnp.where(keep[:, None, None, :], picked, 0.0)
    summed = scatter_sum(
        picked.reshape(n_lat, slots_here // n_lat, half, 2 * degree_count), "lat"
    )
    degree_float = degrees.astype(jnp.float32)
    pair = jnp.concatenate([degree_float, degree_float])
    damping = 1.0 + helm_coef[None, :, None] * (pair * (pair + 1.0))[None, None, :]
    return jnp.transpose(summed / damping, (1, 0, 2))[:, None, :, :]


def solution(mesh):
    block = P("fold", None, "lat", "lon")
    in_specs = (block,) * 5 + (P(), P("lon", "lat", None), P("fold"))
    out_specs = P("fold", "lon", "lat", None)
    return jax.shard_map(local, mesh=mesh, in_specs=in_specs, out_specs=out_specs, check_vma=False)
```

profile of v0, /device:TPU:1, one launch (start us, length us, event | category | flops | bytes accessed | tf_op | source)
XLA Modules:
  0.0 193.0 jit_solution(3154395180186357689)
XLA Ops:
  0.0 8.0 %copy.45 = f32[1,12,160,640]{2,3,1,0:T(8,128)} copy(f32[1,12,160,640]{3,2,1,0:T(8,128)} %param.8) | data formatting | bytes 9830400 | tf_op args[0]
  8.0 7.6 %fusion.23 = (f32[12,8,640]{1,2,0:T(8,128)}, f32[12,8,640]{1,2,0:T(8,128)}) fusion(f32[12,160,640]{1,2,0:T(8,128)} %bitcast.63), kind=kLoop, calls=%fused_computation.51 | loop fusion | bytes 983040 | tf_op jit(solution)/shard_map/slice | solution.py:189
  15.5 3.3 %copy.46 = f32[12,8,640]{2,1,0:T(8,128)} copy(f32[12,8,640]{1,2,0:T(8,128)} %get-tuple-element.8) | data formatting | bytes 491520 | tf_op jit(solution)/shard_map/slice | solution.py:189
  18.9 4.7 %collective-permute-start = (f32[12,8,640]{2,1,0:T(8,128)}, f32[12,8,640]{2,1,0:T(8,128)}, u32[]{:S(2)}, u32[]{:S(2)}) collective-permute-start(f32[12,8,640]{2,1,0:T(8,128)} %copy.46), channel_id=1, source_target_pairs={{0,8},{8,16},{16,24},{1,9},{9,17},{17,25},{2,10},{10,18},{18,26},{... | collective-permute-start | bytes 737288 | tf_op jit(solution)/shard_map/ppermute | solution.py:190
  24.9 3.3 %copy.47 = f32[12,8,640]{2,1,0:T(8,128)} copy(f32[12,8,640]{1,2,0:T(8,128)} %get-tuple-element.7) | data formatting | bytes 491520 | tf_op jit(solution)/shard_map/slice | solution.py:189
  32.4 1.8 subtract_convert_fusion
  34.2 1.6 fusion.22
  36.8 1.5 fusion.27
  39.9 1.5 rev.6
  41.4 1.5 fusion.26
  44.4 1.5 fusion.25
  48.2 1.7 maximum_bitcast_fusion.3
  52.6 1.5 rev.7
  60.0 1.7 maximum_bitcast_fusion.table
  62.9 94.4 %shard_map.82 = f32[12,4,8,160]{3,2,1,0:T(8,128)} custom-call(s32[1]{0:T(128)} %bitcast.2.last, f32[12,160,640]{2,1,0:T(8,128)} %bitcast.65, f32[12,8,640]{2,1,0:T(8,128)} %collective-permute-done.north, f32[12,8,640]{2,1,0:T(8,128)} %collective-permute-done.1.below, f32[12,8,640]{2,1,0:T(8,128)} %collective-permute-done.2.mirror, ...), custom_call_target="tpu_custom_call" | custom-call | tf_op jit(solution)/shard_map/pallas_call | solution.py:155
  157.3 1.7 dynamic-slice_bitcast_fusion.2
  159.0 2.1 %collective-permute-start.7 = (f32[12,8,160]{2,1,0:T(8,128)}, f32[12,8,160]{2,1,0:T(8,128)S(1)}, u32[]{:S(2)}, u32[]{:S(2)}) collective-permute-start(f32[12,8,160]{2,1,0:T(8,128)} %get-tuple-element.12), channel_id=1, source_target_pairs={{0,6},{2,0},{4,2},{6,4},{1,7},{3,1},{5,3},{7,5},{8,14},{10,8},{12,... | collective-permute-start | bytes 184328 | tf_op jit(solution)/shard_map/ppermute | solution.py:213
  165.4 2.4 %collective-permute-done.5 = f32[12,8,160]{2,1,0:T(8,128)} collective-permute-done((f32[12,8,160]{2,1,0:T(8,128)}, f32[12,8,160]{2,1,0:T(8,128)}, u32[]{:S(2)}, u32[]{:S(2)}) %collective-permute-start.5) | collective-permute-done | bytes 61472 | tf_op jit(solution)/shard_map/ppermute | solution.py:213
  168.8 3.4 %collective-permute-start.8 = (f32[6,8,160]{2,1,0:T(8,128)S(1)}, f32[6,8,160]{2,1,0:T(8,128)S(1)}, u32[]{:S(2)}, u32[]{:S(2)}) collective-permute-start(f32[6,8,160]{2,1,0:T(8,128)S(1)} %constant_dynamic-slice_fusion), channel_id=1, source_target_pairs={{0,1},{1,0},{2,3},{3,2},{4,5},{5,4},{6,7},{7,6},{8,9},{9,8},{10,11... | collective-permute-start | bytes 92168 | tf_op jit(solution)/shard_map/ppermute | solution.py:243
  173.2 1.9 fusion.2
  177.9 1.8 copy.63
  179.7 1.9 squeeze.57
  182.8 4.4 %collective-permute-start.11 = (f32[1,6,2560]{2,0,1:T(1,128)S(1)}, f32[1,6,2560]{2,0,1:T(1,128)S(1)}, u32[]{:S(2)}, u32[]{:S(2)}) collective-permute-start(f32[1,6,2560]{2,0,1:T(1,128)S(1)} %get-tuple-element.15), channel_id=1, source_target_pairs={{0,24},{8,0},{16,8},{24,16},{1,25},{9,1},{17,9},{25,17},{2,26},{10... | collective-permute-start | bytes 184328 | tf_op jit(solution)/shard_map/ppermute | solution.py:213
  188.6 3.0 %collective-permute-done.10 = f32[1,6,2560]{2,0,1:T(1,128)S(1)} collective-permute-done((f32[1,6,2560]{2,0,1:T(1,128)S(1)}, f32[1,6,2560]{2,0,1:T(1,128)S(1)}, u32[]{:S(2)}, u32[]{:S(2)}) %collective-permute-start.10) | collective-permute-done | bytes 61472 | tf_op jit(solution)/shard_map/ppermute | solution.py:213
  (63 shorter events, 34.7 us)
Async XLA Ops:
  0.0 173.2 %copy-start = (f32[4,160,1280]{2,1,0:T(8,128)S(1)}, f32[4,160,1280]{2,1,0:T(8,128)}, u32[]{:S(2)}) copy-start(f32[4,160,1280]{2,1,0:T(8,128)} %param.14) | copy-start | bytes 9830404
  15.5 14.0 %copy-start.3 = (s32[16]{0:T(128)S(1)}, s32[16]{0:T(128)}, u32[]{:S(2)}) copy-start(s32[16]{0:T(128)} %param.13) | copy-start | bytes 196
  18.9 25.5 %collective-permute-start = (f32[12,8,640]{2,1,0:T(8,128)}, f32[12,8,640]{2,1,0:T(8,128)}, u32[]{:S(2)}, u32[]{:S(2)}) collective-permute-start(f32[12,8,640]{2,1,0:T(8,128)} %copy.46), channel_id=1, source_target_pairs={{0,8},{8,16},{16,24},{1,9},{9,17},{17,25},{2,10},{10,18},{18,26},{... | collective-permute-start | bytes 737288 | tf_op jit(solution)/shard_map/ppermute | solution.py:190
  23.6 13.3 %collective-permute-start.2 = (f32[12,8,640]{2,1,0:T(8,128)}, f32[12,8,640]{2,1,0:T(8,128)}, u32[]{:S(2)}, u32[]{:S(2)}) collective-permute-start(f32[12,8,640]{2,1,0:T(8,128)} %copy.46), channel_id=1, source_target_pairs={{24,25},{25,24},{26,27},{27,26},{28,29},{29,28},{30,31},{31,30}} | collective-permute-start | bytes 737288 | tf_op jit(solution)/shard_map/ppermute | solution.py:193
  28.3 13.1 %collective-permute-start.1 = (f32[12,8,640]{2,1,0:T(8,128)}, f32[12,8,640]{2,1,0:T(8,128)}, u32[]{:S(2)}, u32[]{:S(2)}) collective-permute-start(f32[12,8,640]{2,1,0:T(8,128)} %copy.47), channel_id=1, source_target_pairs={{8,0},{16,8},{24,16},{9,1},{17,9},{25,17},{10,2},{18,10},{26,18},{... | collective-permute-start | bytes 737288 | tf_op jit(solution)/shard_map/ppermute | solution.py:191
  49.9 11.8 %collective-permute-start.3 = (f32[12,8,176]{2,1,0:T(8,128)}, f32[12,8,176]{2,1,0:T(8,128)}, u32[]{:S(2)}, u32[]{:S(2)}) collective-permute-start(f32[12,8,176]{2,1,0:T(8,128)} %maximum_bitcast_fusion.3), channel_id=1, source_target_pairs={{0,2},{2,4},{4,6},{6,0},{1,3},{3,5},{5,7},{7,1},{8,10},{10,12},{12... | collective-permute-start | bytes 202760 | tf_op jit(solution)/shard_map/ppermute | solution.py:201
  58.8 3.5 %collective-permute-start.4 = (f32[12,8,176]{2,1,0:T(8,128)S(1)}, f32[12,8,176]{2,1,0:T(8,128)S(1)}, u32[]{:S(2)}, u32[]{:S(2)}) collective-permute-start(f32[12,8,176]{2,1,0:T(8,128)S(1)} %maximum_bitcast_fusion.4), channel_id=1, source_target_pairs={{2,0},{4,2},{6,4},{0,6},{3,1},{5,3},{7,5},{1,7},{10,8},{12,10},{14... | collective-permute-start | bytes 202760 | tf_op jit(solution)/shard_map/ppermute | solution.py:202
  62.3 0.6 copy-start.1
  159.0 4.3 %collective-permute-start.7 = (f32[12,8,160]{2,1,0:T(8,128)}, f32[12,8,160]{2,1,0:T(8,128)S(1)}, u32[]{:S(2)}, u32[]{:S(2)}) collective-permute-start(f32[12,8,160]{2,1,0:T(8,128)} %get-tuple-element.12), channel_id=1, source_target_pairs={{0,6},{2,0},{4,2},{6,4},{1,7},{3,1},{5,3},{7,5},{8,14},{10,8},{12,... | collective-permute-start | bytes 184328 | tf_op jit(solution)/shard_map/ppermute | solution.py:213
  161.1 3.7 %collective-permute-start.6 = (f32[12,8,160]{2,1,0:T(8,128)}, f32[12,8,160]{2,1,0:T(8,128)S(1)}, u32[]{:S(2)}, u32[]{:S(2)}) collective-permute-start(f32[12,8,160]{2,1,0:T(8,128)} %get-tuple-element.13), channel_id=1, source_target_pairs={{0,4},{2,6},{4,0},{6,2},{1,5},{3,7},{5,1},{7,3},{8,12},{10,14},{12... | collective-permute-start | bytes 184328 | tf_op jit(solution)/shard_map/ppermute | solution.py:213
  162.3 5.4 %collective-permute-start.5 = (f32[12,8,160]{2,1,0:T(8,128)}, f32[12,8,160]{2,1,0:T(8,128)}, u32[]{:S(2)}, u32[]{:S(2)}) collective-permute-start(f32[12,8,160]{2,1,0:T(8,128)} %get-tuple-element.11), channel_id=1, source_target_pairs={{0,2},{2,4},{4,6},{6,0},{1,3},{3,5},{5,7},{7,1},{8,10},{10,12},{12... | collective-permute-start | bytes 184328 | tf_op jit(solution)/shard_map/ppermute | solution.py:213
  164.8 0.6 copy-start.2
  168.8 4.3 %collective-permute-start.8 = (f32[6,8,160]{2,1,0:T(8,128)S(1)}, f32[6,8,160]{2,1,0:T(8,128)S(1)}, u32[]{:S(2)}, u32[]{:S(2)}) collective-permute-start(f32[6,8,160]{2,1,0:T(8,128)S(1)} %constant_dynamic-slice_fusion), channel_id=1, source_target_pairs={{0,1},{1,0},{2,3},{3,2},{4,5},{5,4},{6,7},{7,6},{8,9},{9,8},{10,11... | collective-permute-start | bytes 92168 | tf_op jit(solution)/shard_map/ppermute | solution.py:243
  173.2 19.1 %copy-start.4 = (f32[6]{0:T(128)S(1)}, f32[6]{0:T(128)}, u32[]{:S(2)}) copy-start(f32[6]{0:T(128)} %param.15) | copy-start | bytes 76
  182.8 5.7 %collective-permute-start.11 = (f32[1,6,2560]{2,0,1:T(1,128)S(1)}, f32[1,6,2560]{2,0,1:T(1,128)S(1)}, u32[]{:S(2)}, u32[]{:S(2)}) collective-permute-start(f32[1,6,2560]{2,0,1:T(1,128)S(1)} %get-tuple-element.15), channel_id=1, source_target_pairs={{0,24},{8,0},{16,8},{24,16},{1,25},{9,1},{17,9},{25,17},{2,26},{10... | collective-permute-start | bytes 184328 | tf_op jit(solution)/shard_map/ppermute | solution.py:213
  187.3 4.3 %collective-permute-start.10 = (f32[1,6,2560]{2,0,1:T(1,128)S(1)}, f32[1,6,2560]{2,0,1:T(1,128)S(1)}, u32[]{:S(2)}, u32[]{:S(2)}) collective-permute-start(f32[1,6,2560]{2,0,1:T(1,128)S(1)} %get-tuple-element.16), channel_id=1, source_target_pairs={{0,16},{8,24},{16,0},{24,8},{1,17},{9,25},{17,1},{25,9},{2,18},{10... | collective-permute-start | bytes 184328 | tf_op jit(solution)/shard_map/ppermute | solution.py:213
  187.3 5.0 %collective-permute-start.9 = (f32[1,6,2560]{2,0,1:T(1,128)S(1)}, f32[1,6,2560]{2,0,1:T(1,128)S(1)}, u32[]{:S(2)}, u32[]{:S(2)}) collective-permute-start(f32[1,6,2560]{2,0,1:T(1,128)S(1)} %get-tuple-element.14), channel_id=1, source_target_pairs={{0,8},{8,16},{16,24},{24,0},{1,9},{9,17},{17,25},{25,1},{2,10},{10... | collective-permute-start | bytes 184328 | tf_op jit(solution)/shard_map/ppermute | solution.py:213
where the time goes:
time: 196 us; the launch traced here: 193 us
  Pallas kernels  94.4 us (48%)
  local copies, waits for them, and re-layouts  53 us (27%)
  starting transfers between devices  21.3 us (11%)
  other arithmetic  11.5 us (6%)
  waiting for transfers between devices  10.8 us (6%)
    pallas_call x1, Pallas kernels, interpolated_waves(): pl.pallas_call(functools.partial(interp_kernel, margin), grid=(levels,),...  94.4 us
    unnamed x17, local copies, waits for them, and re-layouts  18.2 us
    slice x3, local copies, waits for them, and re-layouts, halos_of(): head, tail = (grid[:, :HEAD], grid[:, rows - HEAD:])  14.2 us
    ppermute x6, waiting for transfers between devices, scatter_sum(): lax.ppermute(piece, axis, [(i, (i + step) % count) for i in range(count)])  9.27 us
    ppermute x6, starting transfers between devices, scatter_sum(): lax.ppermute(piece, axis, [(i, (i + step) % count) for i in range(count)])  8.1 us
    ppermute x1, starting transfers between devices, halos_of(): north = lax.ppermute(tail, 'lat', [(i, i + 1) for i in range(last)])  4.71 us
  transfers between devices with their start and end apart: 12, of which 8 were waited for; matrix products, arithmetic and copies ran while one was open for 14% of the time, Pallas kernels for 0%

commit v1 on v0

v1 whole, which is shorter than its diff:
```python
import functools
import math

import jax
import jax.numpy as jnp
from jax import lax
from jax.experimental import pallas as pl
from jax.experimental.pallas import tpu as pltpu
from jax.sharding import PartitionSpec as P

SHIFT_MAX = 4
LANES = 128
SUBS = 8
TAPS = range(-1 - SHIFT_MAX, SHIFT_MAX + 3)
SLOTS = LANES // SUBS


def cubic_weights(t):
    tm, tp, td = t - 1.0, t + 1.0, t - 2.0
    outer = t * tm
    inner = tp * td
    return (
        outer * (td * (-1.0 / 6.0)),
        inner * (tm * 0.5),
        inner * (t * -0.5),
        outer * (tp * (1.0 / 6.0)),
    )


def gather_rows(x, index):
    dims = lax.GatherDimensionNumbers(
        offset_dims=(),
        collapsed_slice_dims=(0,),
        start_index_map=(0,),
        operand_batching_dims=(1,),
        start_indices_batching_dims=(1,),
    )
    mode = lax.GatherScatterMode.PROMISE_IN_BOUNDS
    return lax.gather(x, index[..., None], dims, (1, 1), mode=mode)


def interp_kernel(
    field,
    north,
    south,
    west,
    east,
    corners_west,
    corners_east,
    row_shift,
    col_shift,
    row_frac,
    col_frac,
    table,
    out,
    source_even,
    source_odd,
    grid,
):
    step = pl.program_id(0)
    levels = pl.num_programs(0) - 1
    rows, cols = field.shape[1:]
    count = cols // LANES
    blocks = rows // SUBS
    lane = lax.broadcasted_iota(jnp.int32, (SUBS, LANES), 1)
    sub = lax.broadcasted_iota(jnp.int32, (SUBS, LANES), 0)

    def spread(store, block, middle, left, right):
        at = pl.ds(pl.multiple_of(SUBS * block, SUBS), SUBS)
        tiles = [left, *middle, right]
        for c, move in enumerate(TAPS):
            side = (move > 0) - (move < 0)
            lowest = 1 + min(0, side)
            near = tiles[lowest : lowest + count + abs(side)]
            if side:
                near = [pltpu.roll(x, -move % LANES, 1) for x in near]
            for t in range(count):
                if side > 0:
                    moved = jnp.where(lane < LANES - move, near[t], near[t + 1])
                elif side < 0:
                    moved = jnp.where(lane >= -move, near[t + 1], near[t])
                else:
                    moved = near[t]
                store[c, t, at, :] = moved

    def tiles_of(ref, at):
        return [ref[0, at, t * LANES : (t + 1) * LANES] for t in range(count)]

    def own(store, j):
        at = pl.ds(pl.multiple_of(SUBS * j, SUBS), SUBS)
        group, place = j // SLOTS, SUBS * (j % SLOTS)
        left = pltpu.roll(west[0, group], LANES - SUBS - place, 1)
        right = pltpu.roll(east[0, group], (LANES - place) % LANES, 1)
        spread(store, j + 1, tiles_of(field, at), left, right)

    def beyond(store):
        level = jnp.minimum(step, levels - 1)
        group, place = level // SLOTS, SUBS * (level % SLOTS)
        for end, (block, ref) in enumerate(((0, north), (blocks + 1, south))):
            left = pltpu.roll(corners_west[end, group], LANES - SUBS - place, 1)
            right = pltpu.roll(corners_east[end, group], (LANES - place) % LANES, 1)
            spread(store, block, tiles_of(ref, slice(0, SUBS)), left, right)

    def interpolate(store, j, t):
        at = pl.ds(pl.multiple_of(SUBS * j, SUBS), SUBS)
        cut = slice(t * LANES, (t + 1) * LANES)
        row_t = row_frac[0, at, cut].astype(jnp.float32)
        col_t = col_frac[0, at, cut].astype(jnp.float32)
        weights = cubic_weights(row_t)
        place = sub + (row_shift[0, at, cut] + SHIFT_MAX)
        low = place < SUBS
        index = place & (SUBS - 1)
        left = col_shift[0, at, cut] + SHIFT_MAX
        far = left >= SHIFT_MAX + 1
        near = jnp.where(far, left - SHIFT_MAX, left)

        def column(c):
            picked = []
            for a in range(4):
                base = SUBS * j + (SUBS - SHIFT_MAX - 1 + a)
                upper = gather_rows(store[c, t, pl.ds(base, SUBS), :], index)
                lower = gather_rows(store[c, t, pl.ds(base + SUBS, SUBS), :], index)
                picked.append(jnp.where(low, upper, lower))
            return picked

        def combine(picked):
            total = weights[0] * picked[0]
            for a in range(1, 4):
                total = total + weights[a] * picked[a]
            return total

        columns = {}
        lines = []
        for c in range(SHIFT_MAX + 4):
            for need in (c, c + SHIFT_MAX):
                if need not in columns:
                    columns[need] = column(need)
            both = zip(columns[c], columns[c + SHIFT_MAX])
            lines.append(combine([jnp.where(far, b, a) for a, b in both]))
        most = near >= 3
        lines = [jnp.where(most, lines[i + 2], lines[i]) for i in range(6)]
        near = jnp.where(most, near - 2, near)
        lines = [jnp.where(near >= 2, lines[i + 1], lines[i]) for i in range(5)]
        lines = [jnp.where(near >= 1, lines[i + 1], lines[i]) for i in range(4)]
        slopes = [lines[i + 1] - lines[i] for i in range(3)]
        bend = slopes[1] - slopes[0]
        twist = slopes[2] - slopes[1] - bend
        inner = bend + (col_t * (1.0 / 3.0) + (1.0 / 3.0)) * twist
        grid[at, cut] = lines[1] + col_t * (slopes[1] + (col_t * 0.5 - 0.5) * inner)

    def transform():
        half = table.shape[1] // 2
        values = grid[...]
        top = values.astype(jnp.bfloat16)
        rest = (values - top.astype(jnp.float32)).astype(jnp.bfloat16)
        both = jnp.dot(top, table[...], preferred_element_type=jnp.float32)
        more = jnp.dot(rest, table[:, :half], preferred_element_type=jnp.float32)
        sums = both[:, :half] + both[:, half:] + more
        out[0] = sums.T.reshape(out.shape[1:])

    def run(read, write):
        def body(j, carry):
            own(write, j)
            for t in range(count):
                interpolate(read, j, t)
            return carry

        lax.fori_loop(0, blocks, body, 0)
        beyond(write)
        transform()

    @pl.when(step == 0)
    def _():
        def first(j, carry):
            own(source_even, j)
            return carry

        lax.fori_loop(0, blocks, first, 0)
        beyond(source_even)

    @pl.when((step > 0) & (step % 2 == 1))
    def _():
        run(source_even, source_odd)

    @pl.when((step > 0) & (step % 2 == 0))
    def _():
        run(source_odd, source_even)


def interpolated_waves(field, halos, shifts, fracs, table, n_lon):
    levels, rows, cols = field.shape
    count = cols // LANES

    def per_level(x, level):
        tail = (0,) * (x.ndim - 1)
        return pl.BlockSpec((1,) + x.shape[1:], lambda i: (level(i),) + tail)

    def ahead(x):
        return per_level(x, lambda i: jnp.minimum(i, levels - 1))

    def behind(x):
        return per_level(x, lambda i: jnp.maximum(i - 1, 0))

    def whole(x):
        return pl.BlockSpec(x.shape, lambda i: (0,) * x.ndim)

    north, south, west, east, corners_west, corners_east = halos
    shape = (levels, n_lon, table.shape[1] // 2 // n_lon, rows)
    store = pltpu.VMEM((len(TAPS), count, rows + 2 * SUBS, LANES), jnp.float32)
    return pl.pallas_call(
        interp_kernel,
        grid=(levels + 1,),
        in_specs=[ahead(x) for x in (field, north, south, west, east)]
        + [whole(corners_west), whole(corners_east)]
        + [behind(x) for x in (*shifts, *fracs)]
        + [whole(table)],
        out_specs=pl.BlockSpec((1,) + shape[1:], lambda i: (jnp.maximum(i - 1, 0), 0, 0, 0)),
        out_shape=jax.ShapeDtypeStruct(shape, jnp.float32),
        scratch_shapes=[store, store, pltpu.VMEM((rows, cols), jnp.float32)],
    )(field, north, south, west, east, corners_west, corners_east, *shifts, *fracs, table)


def packed(strip):
    levels, span = strip.shape[:2]
    rows = span - 2 * SUBS

    def lanes_of(pieces):
        front, number = pieces.shape[0], pieces.shape[1]
        groups = -(-number // SLOTS)
        pieces = jnp.pad(pieces, ((0, 0), (0, groups * SLOTS - number), (0, 0), (0, 0)))
        pieces = pieces.reshape(front, groups, SLOTS, SUBS, SUBS)
        return jnp.transpose(pieces, (0, 1, 3, 2, 4)).reshape(front, groups, SUBS, LANES)

    own = lanes_of(strip[:, SUBS:-SUBS].reshape(levels, rows // SUBS, SUBS, SUBS))
    return own, lanes_of(jnp.stack([strip[:, :SUBS], strip[:, -SUBS:]]))


def zonal_table(waves, first_col, cols, lon_total):
    col = first_col + lax.iota(jnp.int32, cols)
    phase = waves[:, None] * col[None, :] % lon_total
    angle = phase.astype(jnp.float32) * (2.0 * math.pi / lon_total)
    pair = jnp.stack([jnp.cos(angle), -jnp.sin(angle)], axis=1) / math.sqrt(lon_total)
    full = pair.reshape(-1, cols)
    top = full.astype(jnp.bfloat16)
    rest = (full - lax.reduce_precision(full, 8, 7)).astype(jnp.bfloat16)
    return jnp.concatenate([top, rest], axis=0).T


def halos_of(grid):
    rows, cols = grid.shape[1:]
    n_lat, n_fold, n_lon = (lax.axis_size(a) for a in ("lat", "fold", "lon"))
    last = n_lat - 1
    at_last = lax.axis_index("lat") == last
    head, tail = grid[:, :SUBS], grid[:, rows - SUBS :]
    north = lax.ppermute(tail, "lat", [(i, i + 1) for i in range(last)])
    below = lax.ppermute(head, "lat", [(i + 1, i) for i in range(last)])
    route = [(last * n_fold + f, last * n_fold + (f ^ 1)) for f in range(n_fold)]
    mirror = lax.ppermute(tail, ("lat", "fold"), route)

    south = jnp.where(at_last, mirror[:, ::-1], below)

    def edge(a, b):
        strip = jnp.concatenate([north[:, :, a:b], grid[:, :, a:b], south[:, :, a:b]], axis=1)
        return jnp.swapaxes(strip, 1, 2)

    ring = [(i, (i + 1) % n_lon) for i in range(n_lon)]
    west = lax.ppermute(edge(cols - SUBS, cols), "lon", ring)
    east = lax.ppermute(edge(0, SUBS), "lon", [(b, a) for a, b in ring])
    west, corners_west = packed(jnp.swapaxes(west, 1, 2))
    east, corners_east = packed(jnp.swapaxes(east, 1, 2))
    return north, south, west, east, corners_west, corners_east


def scatter_sum(pieces, axis):
    count = lax.axis_size(axis)
    place = lax.axis_index(axis)
    total = lax.dynamic_index_in_dim(pieces, place, 0, keepdims=False)
    arrived = []
    for step in range(1, count):
        piece = lax.dynamic_index_in_dim(pieces, (place + step) % count, 0, keepdims=False)
        arrived.append(lax.ppermute(piece, axis, [(i, (i + step) % count) for i in range(count)]))
    for part in arrived:
        total = total + part
    return total


def local(field, row_shift, col_shift, row_frac, col_frac, wave_map, legendre, helm_coef):
    grid = field[0]
    levels, rows, cols = grid.shape
    half = levels // 2
    n_lon, n_lat, n_fold = (lax.axis_size(a) for a in ("lon", "lat", "fold"))
    lon_place = lax.axis_index("lon")
    table = zonal_table(wave_map, lon_place * cols, cols, cols * n_lon)
    halos = halos_of(grid)
    waves_here = interpolated_waves(
        grid,
        halos,
        (row_shift[0], col_shift[0]),
        (row_frac[0], col_frac[0]),
        table,
        n_lon,
    )
    slots_here = wave_map.shape[0] // n_lon
    hemisphere = lax.axis_index("fold") % 2
    sign = (1 - 2 * hemisphere).astype(jnp.float32)
    coeffs = scatter_sum(jnp.swapaxes(waves_here, 0, 1), "lon")
    outgoing = lax.dynamic_slice_in_dim(coeffs, (1 - hemisphere) * half, half, 0)
    incoming = lax.ppermute(outgoing, "fold", [(f, f ^ 1) for f in range(n_fold)])
    kept = lax.dynamic_slice_in_dim(coeffs, hemisphere * half, half, 0)
    folded = jnp.stack([kept + incoming, sign * (kept - incoming)], axis=0)
    folded = jnp.transpose(folded.reshape(2, half, slots_here, 2, rows), (2, 3, 0, 1, 4))
    degree_count = legendre.shape[2]
    degrees = lax.iota(jnp.int32, degree_count)
    waves = lax.dynamic_slice_in_dim(wave_map, lon_place * slots_here, slots_here)
    product = jnp.einsum("sqelk,skn->selqn", folded, legendre, precision=lax.Precision.HIGHEST)
    parity = (waves[:, None] + degrees[None, :]) % 2 == 0
    keep = degrees[None, :] >= waves[:, None]
    picked = jnp.where(parity[:, None, None, :], product[:, 0], product[:, 1])
    picked = jnp.where(keep[:, None, None, :], picked, 0.0)
    summed = scatter_sum(
        picked.reshape(n_lat, slots_here // n_lat, half, 2 * degree_count), "lat"
    )
    degree_float = degrees.astype(jnp.float32)
    pair = jnp.concatenate([degree_float, degree_float])
    damping = 1.0 + helm_coef[None, :, None] * (pair * (pair + 1.0))[None, None, :]
    return jnp.transpose(summed / damping, (1, 0, 2))[:, None, :, :]


def solution(mesh):
    block = P("fold", None, "lat", "lon")
    in_specs = (block,) * 5 + (P(), P("lon", "lat", None), P("fold"))
    out_specs = P("fold", "lon", "lat", None)
    return jax.shard_map(local, mesh=mesh, in_specs=in_specs, out_specs=out_specs, check_vma=False)
```

time: 196 us -> 173 us (0.88)
  Pallas kernels: 94.4 us -> 62.7 us
  local copies, waits for them, and re-layouts: 53 us -> 63.3 us
    pallas_call x1, Pallas kernels: 94.4 us -> 62.7 us  [interpolated_waves(): pl.pallas_call(interp_kernel, grid=(levels + 1,), in_specs=[ahead(x) for...]
    unnamed x17 -> x12, local copies, waits for them, and re-layouts: 18.2 us -> 0.66 us
    reshape x0 -> x6, local copies, waits for them, and re-layouts: none -> 14.3 us  [the longest x4 8.5 us: lanes_of(): jnp.transpose(pieces, (0, 1, 3, 2, 4)).reshape(front, groups, SUBS, LANES)]
    transpose x0 -> x2, local copies, waits for them, and re-layouts: none -> 5.15 us  [lanes_of(): jnp.transpose(pieces, (0, 1, 3, 2, 4)).reshape(front, groups, SUBS, LANES)]
    pad x0 -> x2, local copies, waits for them, and re-layouts: none -> 4.38 us  [lanes_of(): jnp.pad(pieces, ((0, 0), (0, groups * SLOTS - number), (0, 0), (0, 0)))]
    slice x7 -> x14, local copies, waits for them, and re-layouts: 20.4 us -> 23.5 us  [the longest x3 7.72 us: edge(): grid[:, :, a:b]]
    ppermute x6, waiting for transfers between devices: 9.27 us -> 6.8 us  [scatter_sum(): lax.ppermute(piece, axis, [(i, (i + step) % count) for i in range(count)])]
    reshape x0 -> x2, other arithmetic: none -> 2.13 us  [lanes_of(): jnp.transpose(pieces, (0, 1, 3, 2, 4)).reshape(front, groups, SUBS, LANES)]
  transfers between devices with their start and end apart: 12 -> 12, of which waited for: 8 -> 7; matrix products, arithmetic and copies ran while one was open for 14% -> 15% of each run, Pallas kernels for 0% -> 0%
where the time goes in v1:
time: 173 us; the launch traced here: 170 us
  local copies, waits for them, and re-layouts  63.3 us (37%)
  Pallas kernels  62.7 us (36%)
  starting transfers between devices  20.9 us (12%)
  other arithmetic  11.6 us (7%)
  waiting for transfers between devices  9.51 us (5%)
  matrix products  1.92 us (1%)
    pallas_call x1, Pallas kernels, interpolated_waves(): pl.pallas_call(interp_kernel, grid=(levels + 1,), in_specs=[ahead(x) for...  62.7 us
    reshape x4, local copies, waits for them, and re-layouts, lanes_of(): jnp.transpose(pieces, (0, 1, 3, 2, 4)).reshape(front, groups, SUBS, LANES)  8.5 us
    ppermute x6, starting transfers between devices, scatter_sum(): lax.ppermute(piece, axis, [(i, (i + step) % count) for i in range(count)])  7.81 us
    slice x3, local copies, waits for them, and re-layouts, edge(): grid[:, :, a:b]  7.72 us
    ppermute x6, waiting for transfers between devices, scatter_sum(): lax.ppermute(piece, axis, [(i, (i + step) % count) for i in range(count)])  6.8 us
    reshape x2, local copies, waits for them, and re-layouts, lanes_of(): pieces = pieces.reshape(front, groups, SLOTS, SUBS, SUBS)  5.84 us
    slice x4, local copies, waits for them, and re-layouts, packed(): strip[:, SUBS:-SUBS].reshape(levels, rows // SUBS, SUBS, SUBS)  5.52 us
    transpose x2, local copies, waits for them, and re-layouts, lanes_of(): jnp.transpose(pieces, (0, 1, 3, 2, 4)).reshape(front, groups, SUBS, LANES)  5.15 us
  transfers between devices with their start and end apart: 12, of which 7 were waited for; matrix products, arithmetic and copies ran while one was open for 15% of the time, Pallas kernels for 0%

profile of v1, /device:TPU:1, one launch (start us, length us, event | category | flops | bytes accessed | tf_op | source)
XLA Modules:
  0.0 170.2 jit_solution(8768738686786360998)
XLA Ops:
  0.0 2.0 %fusion.25 = (f32[12,8,640]{2,1,0:T(8,128)}, f32[12,8,640]{2,1,0:T(8,128)}) fusion(f32[12,160,640]{2,1,0:T(8,128)} %bitcast.93), kind=kLoop, calls=%fused_computation.59 | loop fusion | bytes 983040 | tf_op jit(solution)/shard_map/slice | solution.py:254
  3.4 4.7 %collective-permute-start = (f32[12,8,640]{2,1,0:T(8,128)}, f32[12,8,640]{2,1,0:T(8,128)}, u32[]{:S(2)}, u32[]{:S(2)}) collective-permute-start(f32[12,8,640]{2,1,0:T(8,128)} %get-tuple-element.8), channel_id=1, source_target_pairs={{0,8},{8,16},{16,24},{1,9},{9,17},{17,25},{2,10},{10,18},{18,26},{... | collective-permute-start | bytes 737288 | tf_op jit(solution)/shard_map/ppermute | solution.py:255
  11.5 3.2 %fusion.24 = (f32[12,160,8]{2,1,0:T(8,128)}, f32[12,160,8]{2,1,0:T(8,128)}) fusion(f32[12,160,640]{2,1,0:T(8,128)} %bitcast.94), kind=kLoop, calls=%fused_computation.58 | loop fusion | bytes 245760 | tf_op jit(solution)/shard_map/slice | solution.py:263
  15.7 2.3 %copy.78 = f32[12,160,8]{1,2,0:T(8,128)} copy(f32[12,160,8]{2,1,0:T(8,128)} %get-tuple-element.5) | data formatting | bytes 122880 | tf_op jit(solution)/shard_map/slice | solution.py:263
  18.0 2.3 %copy.72 = f32[12,160,8]{1,2,0:T(8,128)} copy(f32[12,160,8]{2,1,0:T(8,128)} %get-tuple-element.6) | data formatting | bytes 122880 | tf_op jit(solution)/shard_map/slice | solution.py:263
  22.2 3.1 %rev.3 = f32[12,8,640]{2,1,0:T(8,128)} reverse(f32[12,8,640]{2,1,0:T(8,128)} %collective-permute-done.1), dimensions={1} | reverse | bytes 491520 | tf_op jit(solution)/shard_map/rev | solution.py:260
  33.2 2.2 %collective-permute-start.4 = (f32[12,8,176]{2,1,0:T(8,128)}, f32[12,8,176]{2,1,0:T(8,128)}, u32[]{:S(2)}, u32[]{:S(2)}) collective-permute-start(f32[12,8,176]{2,1,0:T(8,128)} %maximum_bitcast_fusion.4), channel_id=1, source_target_pairs={{2,0},{4,2},{6,4},{0,6},{3,1},{5,3},{7,5},{1,7},{10,8},{12,10},{14... | collective-permute-start | bytes 202760 | tf_op jit(solution)/shard_map/ppermute | solution.py:268
  50.5 2.0 %copy.80 = f32[12,160,8]{0,2,1:T(8,128)} copy(f32[12,160,8]{1,2,0:T(8,128)} %slice.73) | data formatting | bytes 122880 | tf_op jit(solution)/shard_map/slice | solution.py:234
  52.5 2.2 %pad.15 = f32[12,32,8,8]{0,3,2,1:T(8,128)} pad(f32[12,20,8,8]{0,3,2,1:T(8,128)} %bitcast.103, f32[]{:T(128)} %constant.108.clone.1), padding=0_0x0_12x0_0x0_0 | pad | bytes 159748 | tf_op jit(solution)/shard_map/jit(_pad)/pad | solution.py:230
  54.7 2.9 %copy.97 = f32[12,2,16,8,8]{2,1,4,3,0:T(2,128)} copy(f32[12,2,16,8,8]{0,4,3,2,1:T(8,128)} %bitcast.99) | data formatting | bytes 196608 | tf_op jit(solution)/shard_map/reshape | solution.py:231
  57.7 2.6 %copy.82 = f32[12,2,8,16,8]{4,3,2,1,0:T(8,128)} copy(f32[12,2,8,16,8]{3,1,4,2,0:T(2,128)} %bitcast.100) | data formatting | bytes 196608 | tf_op jit(solution)/shard_map/transpose | solution.py:232
  60.3 2.7 %reshape.301.east = f32[12,2,8,128]{3,2,1,0:T(8,128)} reshape(f32[12,2,8,16,8]{4,3,2,1,0:T(8,128)} %copy.82) | data formatting | bytes 196608 | tf_op jit(solution)/shard_map/reshape | solution.py:232
  64.1 2.2 %pad.14 = f32[12,32,8,8]{0,3,2,1:T(8,128)} pad(f32[12,20,8,8]{0,3,2,1:T(8,128)} %bitcast.102, f32[]{:T(128)} %constant.108.clone.1), padding=0_0x0_12x0_0x0_0 | pad | bytes 159748 | tf_op jit(solution)/shard_map/jit(_pad)/pad | solution.py:230
  66.3 2.9 %copy.96 = f32[12,2,16,8,8]{2,1,4,3,0:T(2,128)} copy(f32[12,2,16,8,8]{0,4,3,2,1:T(8,128)} %bitcast.98) | data formatting | bytes 196608 | tf_op jit(solution)/shard_map/reshape | solution.py:231
  69.2 2.6 %copy.76 = f32[12,2,8,16,8]{4,3,2,1,0:T(8,128)} copy(f32[12,2,8,16,8]{3,1,4,2,0:T(2,128)} %bitcast.101) | data formatting | bytes 196608 | tf_op jit(solution)/shard_map/transpose | solution.py:232
  71.7 2.7 %reshape.298.west = f32[12,2,8,128]{3,2,1,0:T(8,128)} reshape(f32[12,2,8,16,8]{4,3,2,1,0:T(8,128)} %copy.76) | data formatting | bytes 196608 | tf_op jit(solution)/shard_map/reshape | solution.py:232
  74.4 62.7 %shard_map.82 = f32[12,4,8,160]{3,2,1,0:T(8,128)} custom-call(f32[12,160,640]{2,1,0:T(8,128)} %bitcast.95, f32[12,8,640]{2,1,0:T(8,128)} %collective-permute-done.north, f32[12,8,640]{2,1,0:T(8,128)} %copy-done.1, f32[12,2,8,128]{3,2,1,0:T(8,128)} %reshape.298.west, f32[12,2,8,128]{3,2,1,0:T(8,128)} %reshape.301.east, f32[2,1,8,128]{3,2,1,0:T(8,128)} %copy.89.corners_west, ...), custom_call_target="tpu_custom_call" | custom-call | tf_op jit(solution)/shard_map/pallas_call | solution.py:210
  141.6 2.0 %collective-permute-done.5 = f32[12,8,160]{2,1,0:T(8,128)S(1)} collective-permute-done((f32[12,8,160]{2,1,0:T(8,128)}, f32[12,8,160]{2,1,0:T(8,128)S(1)}, u32[]{:S(2)}, u32[]{:S(2)}) %collective-permute-start.5) | collective-permute-done | bytes 61472 | tf_op jit(solution)/shard_map/ppermute | solution.py:281
  145.4 3.5 %collective-permute-start.8 = (f32[6,8,160]{2,1,0:T(8,128)S(1)}, f32[6,8,160]{2,1,0:T(8,128)S(1)}, u32[]{:S(2)}, u32[]{:S(2)}) collective-permute-start(f32[6,8,160]{2,1,0:T(8,128)S(1)} %constant_dynamic-slice_fusion), channel_id=1, source_target_pairs={{0,1},{1,0},{2,3},{3,2},{4,5},{5,4},{6,7},{7,6},{8,9},{9,8},{10,11... | collective-permute-start | bytes 92168 | tf_op jit(solution)/shard_map/ppermute | solution.py:308
  149.8 1.9 %fusion.2 = f32[4,2,6,2,1280]{4,2,1,3,0:T(8,128)S(1)} fusion(f32[4,160,1280]{2,1,0:T(8,128)S(1)} %copy-done, f32[1,6,4,2,160]{4,1,0,3,2:T(8,128)S(1)} %bitcast.109, f32[1,6,4,2,160]{4,1,0,3,2:T(8,128)S(1)} %bitcast.108), kind=kOutput, calls=%fused_computation.2 | convolution fusion | flops 235944960 | bytes 3829760 | tf_op jit(solution)/shard_map/sqelk,skn->selqn/dot_general | solution.py:315
  156.4 1.9 %squeeze.57 = f32[4,1,6,2560]{3,0,2,1:T(4,128)} reshape(f32[4,1,6,2,1280]{4,3,0,2,1:T(2,128)} %copy.94) | data formatting | bytes 491520 | tf_op jit(solution)/shard_map/squeeze | solution.py:318
  159.5 3.1 %collective-permute-start.10 = (f32[1,6,2560]{2,0,1:T(1,128)S(1)}, f32[1,6,2560]{2,0,1:T(1,128)S(1)}, u32[]{:S(2)}, u32[]{:S(2)}) collective-permute-start(f32[1,6,2560]{2,0,1:T(1,128)S(1)} %get-tuple-element.16), channel_id=1, source_target_pairs={{0,16},{8,24},{16,0},{24,8},{1,17},{9,25},{17,1},{25,9},{2,18},{10... | collective-permute-start | bytes 184328 | tf_op jit(solution)/shard_map/ppermute | solution.py:281
  162.6 1.9 %collective-permute-start.11 = (f32[1,6,2560]{2,0,1:T(1,128)S(1)}, f32[1,6,2560]{2,0,1:T(1,128)S(1)}, u32[]{:S(2)}, u32[]{:S(2)}) collective-permute-start(f32[1,6,2560]{2,0,1:T(1,128)S(1)} %get-tuple-element.15), channel_id=1, source_target_pairs={{0,24},{8,0},{16,8},{24,16},{1,25},{9,1},{17,9},{25,17},{2,26},{10... | collective-permute-start | bytes 184328 | tf_op jit(solution)/shard_map/ppermute | solution.py:281
  166.3 3.0 %collective-permute-done.9 = f32[1,6,2560]{2,0,1:T(1,128)S(1)} collective-permute-done((f32[1,6,2560]{2,0,1:T(1,128)S(1)}, f32[1,6,2560]{2,0,1:T(1,128)S(1)}, u32[]{:S(2)}, u32[]{:S(2)}) %collective-permute-start.9) | collective-permute-done | bytes 61472 | tf_op jit(solution)/shard_map/ppermute | solution.py:281
  (77 shorter events, 47.4 us)
Async XLA Ops:
  0.0 149.8 %copy-start = (f32[4,160,1280]{2,1,0:T(8,128)S(1)}, f32[4,160,1280]{2,1,0:T(8,128)}, u32[]{:S(2)}) copy-start(f32[4,160,1280]{2,1,0:T(8,128)} %param.14) | copy-start | bytes 9830404
  2.0 20.2 %collective-permute-start.1 = (f32[12,8,640]{2,1,0:T(8,128)}, f32[12,8,640]{2,1,0:T(8,128)}, u32[]{:S(2)}, u32[]{:S(2)}) collective-permute-start(f32[12,8,640]{2,1,0:T(8,128)} %get-tuple-element.8), channel_id=1, source_target_pairs={{24,25},{25,24},{26,27},{27,26},{28,29},{29,28},{30,31},{31,30}} | collective-permute-start | bytes 737288 | tf_op jit(solution)/shard_map/ppermute | solution.py:258
  3.4 25.1 %collective-permute-start = (f32[12,8,640]{2,1,0:T(8,128)}, f32[12,8,640]{2,1,0:T(8,128)}, u32[]{:S(2)}, u32[]{:S(2)}) collective-permute-start(f32[12,8,640]{2,1,0:T(8,128)} %get-tuple-element.8), channel_id=1, source_target_pairs={{0,8},{8,16},{16,24},{1,9},{9,17},{17,25},{2,10},{10,18},{18,26},{... | collective-permute-start | bytes 737288 | tf_op jit(solution)/shard_map/ppermute | solution.py:255
  8.1 17.2 %collective-permute-start.2 = (f32[12,8,640]{2,1,0:T(8,128)}, f32[12,8,640]{2,1,0:T(8,128)}, u32[]{:S(2)}, u32[]{:S(2)}) collective-permute-start(f32[12,8,640]{2,1,0:T(8,128)} %get-tuple-element.7), channel_id=1, source_target_pairs={{8,0},{16,8},{24,16},{9,1},{17,9},{25,17},{10,2},{18,10},{26,18},{... | collective-permute-start | bytes 737288 | tf_op jit(solution)/shard_map/ppermute | solution.py:256
  11.5 8.8 %copy-start.4 = (s32[16]{0:T(128)S(1)}, s32[16]{0:T(128)}, u32[]{:S(2)}) copy-start(s32[16]{0:T(128)} %param.13) | copy-start | bytes 196
  26.3 31.3 %copy-start.1 = (f32[12,8,640]{2,1,0:T(8,128)}, f32[12,8,640]{2,1,0:T(8,128)S(1)}, u32[]{:S(2)}) copy-start(f32[12,8,640]{2,1,0:T(8,128)S(1)} %broadcast_select_fusion.south) | copy-start | bytes 737284
  33.2 6.3 %collective-permute-start.4 = (f32[12,8,176]{2,1,0:T(8,128)}, f32[12,8,176]{2,1,0:T(8,128)}, u32[]{:S(2)}, u32[]{:S(2)}) collective-permute-start(f32[12,8,176]{2,1,0:T(8,128)} %maximum_bitcast_fusion.4), channel_id=1, source_target_pairs={{2,0},{4,2},{6,4},{0,6},{3,1},{5,3},{7,5},{1,7},{10,8},{12,10},{14... | collective-permute-start | bytes 202760 | tf_op jit(solution)/shard_map/ppermute | solution.py:268
  39.4 4.4 %collective-permute-start.3 = (f32[12,8,176]{2,1,0:T(8,128)S(1)}, f32[12,8,176]{2,1,0:T(8,128)S(1)}, u32[]{:S(2)}, u32[]{:S(2)}) collective-permute-start(f32[12,8,176]{2,1,0:T(8,128)S(1)} %maximum_bitcast_fusion.3), channel_id=1, source_target_pairs={{0,2},{2,4},{4,6},{6,0},{1,3},{3,5},{5,7},{7,1},{8,10},{10,12},{12... | collective-permute-start | bytes 202760 | tf_op jit(solution)/shard_map/ppermute | solution.py:267
  57.7 5.3 %copy-start.2 = (f32[12,160,8]{1,2,0:T(8,128)S(1)}, f32[12,160,8]{1,2,0:T(8,128)}, u32[]{:S(2)}) copy-start(f32[12,160,8]{1,2,0:T(8,128)} %slice.69) | copy-start | bytes 184324
  138.9 4.7 %collective-permute-start.5 = (f32[12,8,160]{2,1,0:T(8,128)}, f32[12,8,160]{2,1,0:T(8,128)S(1)}, u32[]{:S(2)}, u32[]{:S(2)}) collective-permute-start(f32[12,8,160]{2,1,0:T(8,128)} %get-tuple-element.11), channel_id=1, source_target_pairs={{0,2},{2,4},{4,6},{6,0},{1,3},{3,5},{5,7},{7,1},{8,10},{10,12},{12... | collective-permute-start | bytes 184328 | tf_op jit(solution)/shard_map/ppermute | solution.py:281
  138.9 4.7 %collective-permute-start.6 = (f32[12,8,160]{2,1,0:T(8,128)}, f32[12,8,160]{2,1,0:T(8,128)S(1)}, u32[]{:S(2)}, u32[]{:S(2)}) collective-permute-start(f32[12,8,160]{2,1,0:T(8,128)} %get-tuple-element.13), channel_id=1, source_target_pairs={{0,4},{2,6},{4,0},{6,2},{1,5},{3,7},{5,1},{7,3},{8,12},{10,14},{12... | collective-permute-start | bytes 184328 | tf_op jit(solution)/shard_map/ppermute | solution.py:281
  139.7 4.7 %collective-permute-start.7 = (f32[12,8,160]{2,1,0:T(8,128)}, f32[12,8,160]{2,1,0:T(8,128)}, u32[]{:S(2)}, u32[]{:S(2)}) collective-permute-start(f32[12,8,160]{2,1,0:T(8,128)} %get-tuple-element.12), channel_id=1, source_target_pairs={{0,6},{2,0},{4,2},{6,4},{1,7},{3,1},{5,3},{7,5},{8,14},{10,8},{12,... | collective-permute-start | bytes 184328 | tf_op jit(solution)/shard_map/ppermute | solution.py:281
  143.6 0.6 copy-start.3
  145.4 4.3 %collective-permute-start.8 = (f32[6,8,160]{2,1,0:T(8,128)S(1)}, f32[6,8,160]{2,1,0:T(8,128)S(1)}, u32[]{:S(2)}, u32[]{:S(2)}) collective-permute-start(f32[6,8,160]{2,1,0:T(8,128)S(1)} %constant_dynamic-slice_fusion), channel_id=1, source_target_pairs={{0,1},{1,0},{2,3},{3,2},{4,5},{5,4},{6,7},{7,6},{8,9},{9,8},{10,11... | collective-permute-start | bytes 92168 | tf_op jit(solution)/shard_map/ppermute | solution.py:308
  151.8 17.6 %copy-start.5 = (f32[6]{0:T(128)S(1)}, f32[6]{0:T(128)}, u32[]{:S(2)}) copy-start(f32[6]{0:T(128)} %param.15) | copy-start | bytes 76
  159.5 5.2 %collective-permute-start.10 = (f32[1,6,2560]{2,0,1:T(1,128)S(1)}, f32[1,6,2560]{2,0,1:T(1,128)S(1)}, u32[]{:S(2)}, u32[]{:S(2)}) collective-permute-start(f32[1,6,2560]{2,0,1:T(1,128)S(1)} %get-tuple-element.16), channel_id=1, source_target_pairs={{0,16},{8,24},{16,0},{24,8},{1,17},{9,25},{17,1},{25,9},{2,18},{10... | collective-permute-start | bytes 184328 | tf_op jit(solution)/shard_map/ppermute | solution.py:281
  162.6 3.7 %collective-permute-start.11 = (f32[1,6,2560]{2,0,1:T(1,128)S(1)}, f32[1,6,2560]{2,0,1:T(1,128)S(1)}, u32[]{:S(2)}, u32[]{:S(2)}) collective-permute-start(f32[1,6,2560]{2,0,1:T(1,128)S(1)} %get-tuple-element.15), channel_id=1, source_target_pairs={{0,24},{8,0},{16,8},{24,16},{1,25},{9,1},{17,9},{25,17},{2,26},{10... | collective-permute-start | bytes 184328 | tf_op jit(solution)/shard_map/ppermute | solution.py:281
  164.5 4.9 %collective-permute-start.9 = (f32[1,6,2560]{2,0,1:T(1,128)S(1)}, f32[1,6,2560]{2,0,1:T(1,128)S(1)}, u32[]{:S(2)}, u32[]{:S(2)}) collective-permute-start(f32[1,6,2560]{2,0,1:T(1,128)S(1)} %get-tuple-element.14), channel_id=1, source_target_pairs={{0,8},{8,16},{16,24},{24,0},{1,9},{9,17},{17,25},{25,1},{2,10},{10... | collective-permute-start | bytes 184328 | tf_op jit(solution)/shard_map/ppermute | solution.py:281

commit v2 on v1

--- a/solution.py
+++ b/solution.py
@@ -220,79 +220,429 @@
     )(field, north, south, west, east, corners_west, corners_east, *shifts, *fracs, table)
 
 
-def packed(strip):
-    levels, span = strip.shape[:2]
-    rows = span - 2 * SUBS
-
-    def lanes_of(pieces):
-        front, number = pieces.shape[0], pieces.shape[1]
-        groups = -(-number // SLOTS)
-        pieces = jnp.pad(pieces, ((0, 0), (0, groups * SLOTS - number), (0, 0), (0, 0)))
-        pieces = pieces.reshape(front, groups, SLOTS, SUBS, SUBS)
-        return jnp.transpose(pieces, (0, 1, 3, 2, 4)).reshape(front, groups, SUBS, LANES)
-
-    own = lanes_of(strip[:, SUBS:-SUBS].reshape(levels, rows // SUBS, SUBS, SUBS))
-    return own, lanes_of(jnp.stack([strip[:, :SUBS], strip[:, -SUBS:]]))
-
-
-def zonal_table(waves, first_col, cols, lon_total):
-    col = first_col + lax.iota(jnp.int32, cols)
-    phase = waves[:, None] * col[None, :] % lon_total
-    angle = phase.astype(jnp.float32) * (2.0 * math.pi / lon_total)
-    pair = jnp.stack([jnp.cos(angle), -jnp.sin(angle)], axis=1) / math.sqrt(lon_total)
-    full = pair.reshape(-1, cols)
-    top = full.astype(jnp.bfloat16)
-    rest = (full - lax.reduce_precision(full, 8, 7)).astype(jnp.bfloat16)
-    return jnp.concatenate([top, rest], axis=0).T
-
-
-def halos_of(grid):
-    rows, cols = grid.shape[1:]
-    n_lat, n_fold, n_lon = (lax.axis_size(a) for a in ("lat", "fold", "lon"))
+MESH = pl.DeviceIdType.MESH
+
+
+def signal_to(semaphore, place):
+    pl.semaphore_signal(semaphore, inc=1, device_id=place, device_id_type=MESH)
+
+
+def remote(source, target, sends, receives, place):
+    return pltpu.make_async_remote_copy(
+        src_ref=source,
+        dst_ref=target,
+        send_sem=sends,
+        recv_sem=receives,
+        device_id=place,
+        device_id_type=MESH,
+    )
+
+
+def halo_kernel(
+    lon_total,
+    field,
+    wave_map,
+    north,
+    south,
+    west,
+    east,
+    corners_west,
+    corners_east,
+    table,
+    edge_west,
+    edge_east,
+    outside,
+    to_west,
+    to_east,
+    corners_to_west,
+    corners_to_east,
+    local_sems,
+    row_sends,
+    north_sem,
+    south_sem,
+    lon_sends,
+    lon_receives,
+):
+    levels, rows, cols = field.shape
+    count = cols // LANES
+    blocks = rows // SUBS
+    n_lat, n_lon = lax.axis_size("lat"), lax.axis_size("lon")
+    lat, lon, fold = (lax.axis_index(a) for a in ("lat", "lon", "fold"))
     last = n_lat - 1
-    at_last = lax.axis_index("lat") == last
-    head, tail = grid[:, :SUBS], grid[:, rows - SUBS :]
-    north = lax.ppermute(tail, "lat", [(i, i + 1) for i in range(last)])
-    below = lax.ppermute(head, "lat", [(i + 1, i) for i in range(last)])
-    route = [(last * n_fold + f, last * n_fold + (f ^ 1)) for f in range(n_fold)]
-    mirror = lax.ppermute(tail, ("lat", "fold"), route)
-
-    south = jnp.where(at_last, mirror[:, ::-1], below)
-
-    def edge(a, b):
-        strip = jnp.concatenate([north[:, :, a:b], grid[:, :, a:b], south[:, :, a:b]], axis=1)
-        return jnp.swapaxes(strip, 1, 2)
-
-    ring = [(i, (i + 1) % n_lon) for i in range(n_lon)]
-    west = lax.ppermute(edge(cols - SUBS, cols), "lon", ring)
-    east = lax.ppermute(edge(0, SUBS), "lon", [(b, a) for a, b in ring])
-    west, corners_west = packed(jnp.swapaxes(west, 1, 2))
-    east, corners_east = packed(jnp.swapaxes(east, 1, 2))
-    return north, south, west, east, corners_west, corners_east
-
-
-def scatter_sum(pieces, axis):
-    count = lax.axis_size(axis)
-    place = lax.axis_index(axis)
-    total = lax.dynamic_index_in_dim(pieces, place, 0, keepdims=False)
-    arrived = []
-    for step in range(1, count):
-        piece = lax.dynamic_index_in_dim(pieces, (place + step) % count, 0, keepdims=False)
-        arrived.append(lax.ppermute(piece, axis, [(i, (i + step) % count) for i in range(count)]))
-    for part in arrived:
-        total = total + part
-    return total
+    hemisphere = fold % 2
+    partner = {"fold": fold + 1 - 2 * hemisphere}
+    eastward = {"lon": lax.rem(lon + 1, n_lon)}
+    westward = {"lon": lax.rem(lon + n_lon - 1, n_lon)}
+    lane = lax.broadcasted_iota(jnp.int32, (SUBS, LANES), 1)
+    sub = lax.broadcasted_iota(jnp.int32, (SUBS, LANES), 0)
+
+    edges = [
+        pltpu.make_async_copy(field.at[:, :, 0:LANES], edge_west, local_sems.at[0]),
+        pltpu.make_async_copy(field.at[:, :, cols - LANES : cols], edge_east, local_sems.at[1]),
+    ]
+    for copy in edges:
+        copy.start()
+
+    barrier = pltpu.get_barrier_semaphore()
+    signal_to(barrier, eastward)
+    signal_to(barrier, westward)
+
+    @pl.when(lat > 0)
+    def _():
+        signal_to(barrier, {"lat": lat - 1})
+
+    @pl.when(lat < last)
+    def _():
+        signal_to(barrier, {"lat": lat + 1})
+
+    @pl.when(lat == last)
+    def _():
+        signal_to(barrier, partner)
+
+    pl.semaphore_wait(barrier, 3 + jnp.minimum(lat, 1))
+
+    head = field.at[:, 0:SUBS, :]
+    tail = field.at[:, rows - SUBS : rows, :]
+
+    def southward():
+        return remote(tail, north, row_sends.at[0], north_sem, {"lat": lat + 1})
+
+    def across():
+        return remote(tail, outside, row_sends.at[0], south_sem, partner)
+
+    def northward():
+        return remote(head, outside, row_sends.at[1], south_sem, {"lat": lat - 1})
+
+    @pl.when(lat < last)
+    def _():
+        southward().start()
+
+    @pl.when(lat == last)
+    def _():
+        across().start()
+
+    @pl.when(lat > 0)
+    def _():
+        northward().start()
+
+    for copy in edges:
+        copy.wait()
+
+    def pack_level(level, carry):
+        for group in range(to_west.shape[1]):
+            first = jnp.zeros((SUBS, LANES), jnp.float32)
+            final = jnp.zeros((SUBS, LANES), jnp.float32)
+            for k in range(min(SLOTS, blocks - group * SLOTS)):
+                at = slice(SUBS * (group * SLOTS + k), SUBS * (group * SLOTS + k + 1))
+                here = (lane >= SUBS * k) & (lane < SUBS * (k + 1))
+                moved = edge_west[level, at, :]
+                if k:
+                    moved = pltpu.roll(moved, SUBS * k, 1)
+                first = jnp.where(here, moved, first)
+                moved = edge_east[level, at, :]
+                if k < SLOTS - 1:
+                    moved = pltpu.roll(moved, SUBS * (k + 1), 1)
+                final = jnp.where(here, moved, final)
+            to_west[level, group] = first
+            to_east[level, group] = final
+        return carry
+
+    lax.fori_loop(0, levels, pack_level, 0)
+
+    strips = [
+        remote(to_west, east, lon_sends.at[0], lon_receives.at[0], westward),
+        remote(to_east, west, lon_sends.at[1], lon_receives.at[1], eastward),
+    ]
+    for copy in strips:
+        copy.start()
+
+    width = table.shape[1] // 2
+    chunk = 2 * SUBS
+    column = lax.broadcasted_iota(jnp.int32, (chunk, 2 * width), 1)
+    which = jnp.where(column < width, column, column - width)
+    slot, part = which >> 1, which & 1
+    wave = jnp.zeros((chunk, 2 * width), jnp.int32)
+    for s in range(width // 2):
+        wave = jnp.where(slot == s, wave_map[s], wave)
+    wave = wave.astype(jnp.float32)
+    quarter = part.astype(jnp.float32) * (lon_total / 4.0)
+    down = lax.broadcasted_iota(jnp.int32, (chunk, 2 * width), 0)
+    start = lon * cols
+
+    def table_rows(i, carry):
+        place = (start + i * chunk + down).astype(jnp.float32)
+        product = wave * place
+        turns = jnp.floor(product * (1.0 / lon_total))
+        phase = product - turns * lon_total + quarter
+        phase = jnp.where(phase < 0.0, phase + lon_total, phase)
+        phase = jnp.where(phase >= lon_total, phase - lon_total, phase)
+        phase = jnp.where(phase >= lon_total, phase - lon_total, phase)
+        value = jnp.cos(phase * (2.0 * math.pi / lon_total)) * (1.0 / math.sqrt(lon_total))
+        top = value.astype(jnp.bfloat16).astype(jnp.float32)
+        both = jnp.where(column < width, top, value - top)
+        table[pl.ds(pl.multiple_of(i * chunk, chunk), chunk), :] = both.astype(jnp.bfloat16)
+        return carry
+
+    lax.fori_loop(0, cols // chunk, table_rows, 0)
+
+    @pl.when(lat > 0)
+    def _():
+        southward().wait_recv()
+
+    @pl.when(lat == 0)
+    def _():
+        north[...] = jnp.zeros(north.shape, jnp.float32)
+
+    across().wait_recv()
+    flip = jnp.where(jnp.full((SUBS, LANES), lat, jnp.int32) == last, SUBS - 1 - sub, sub)
+
+    corners_to_west[...] = jnp.zeros(corners_to_west.shape, jnp.float32)
+    corners_to_east[...] = jnp.zeros(corners_to_east.shape, jnp.float32)
+
+    for level in range(levels):
+        for t in range(count):
+            cut = slice(t * LANES, (t + 1) * LANES)
+            south[level, :, cut] = gather_rows(outside[level, :, cut], flip)
+    for level in range(levels):
+        group, place = level // SLOTS, SUBS * (level % SLOTS)
+        here = (lane >= place) & (lane < place + SUBS)
+        for end, ref in enumerate((north, south)):
+            moved = pltpu.roll(ref[level, :, 0:LANES], place, 1) if place else ref[level, :, 0:LANES]
+            corners_to_west[end, group] = jnp.where(here, moved, corners_to_west[end, group])
+            moved = ref[level, :, cols - LANES : cols]
+            if place < LANES - SUBS:
+                moved = pltpu.roll(moved, place + SUBS, 1)
+            corners_to_east[end, group] = jnp.where(here, moved, corners_to_east[end, group])
+
+    corners = [
+        remote(corners_to_west, corners_east, lon_sends.at[2], lon_receives.at[2], westward),
+        remote(corners_to_east, corners_west, lon_sends.at[3], lon_receives.at[3], eastward),
+    ]
+    for copy in corners:
+        copy.start()
+    for copy in strips + corners:
+        copy.wait()
+    across().wait_send()
+
+    @pl.when(lat > 0)
+    def _():
+        northward().wait_send()
+
+
+def exchanged_halos(field, wave_map, lon_total):
+    levels, rows, cols = field.shape
+    groups = -(-rows // (SUBS * SLOTS))
+    vmem = pl.BlockSpec(memory_space=pltpu.VMEM)
+    rows_shape = (levels, SUBS, cols)
+    strip_shape = (levels, groups, SUBS, LANES)
+    corner_shape = (2, -(-levels // SLOTS), SUBS, LANES)
+    shapes = [rows_shape] * 2 + [strip_shape] * 2 + [corner_shape] * 2
+    f32 = jnp.float32
+    edge = pltpu.VMEM((levels, rows, LANES), f32)
+    return pl.pallas_call(
+        functools.partial(halo_kernel, lon_total),
+        in_specs=[pl.BlockSpec(memory_space=pl.ANY), pl.BlockSpec(memory_space=pltpu.SMEM)],
+        out_specs=[vmem] * 7,
+        out_shape=[jax.ShapeDtypeStruct(s, f32) for s in shapes]
+        + [jax.ShapeDtypeStruct((cols, 4 * wave_map.shape[0]), jnp.bfloat16)],
+        scratch_shapes=[
+            edge,
+            edge,
+            pltpu.VMEM(rows_shape, f32),
+            pltpu.VMEM(strip_shape, f32),
+            pltpu.VMEM(strip_shape, f32),
+            pltpu.VMEM(corner_shape, f32),
+            pltpu.VMEM(corner_shape, f32),
+            pltpu.SemaphoreType.DMA((2,)),
+            pltpu.SemaphoreType.DMA((2,)),
+            pltpu.SemaphoreType.DMA,
+            pltpu.SemaphoreType.DMA,
+            pltpu.SemaphoreType.DMA((4,)),
+            pltpu.SemaphoreType.DMA((4,)),
+        ],
+        compiler_params=pltpu.CompilerParams(collective_id=0, has_side_effects=True),
+    )(field, wave_map)
+
+
+def spectral_kernel(
+    waves,
+    legendre,
+    wave_map,
+    helm,
+    out,
+    matrix,
+    matrix_top,
+    matrix_rest,
+    gathered,
+    left,
+    outgoing,
+    partial,
+    local_sems,
+    zonal_sends,
+    zonal_receives,
+    lat_sends,
+    lat_receives,
+):
+    levels, n_lon, width, rows = waves.shape
+    half = levels // 2
+    slots, _, degrees = legendre.shape
+    n_lat = lax.axis_size("lat")
+    lat, lon, fold = (lax.axis_index(a) for a in ("lat", "lon", "fold"))
+    hemisphere = fold % 2
+    per_lat = slots // n_lat
+
+    load = pltpu.make_async_copy(legendre, matrix, local_sems.at[0])
+    load.start()
+
+    barrier = pltpu.get_barrier_semaphore()
+    peers = [(h, p) for h in range(2) for p in range(n_lon) if h or p]
+
+    def zonal_peer(h, p):
+        other = lax.rem(hemisphere + h, 2)
+        return other, {"lon": lax.rem(lon + p, n_lon), "fold": fold - hemisphere + other}
+
+    def lat_peer(d):
+        return lax.rem(lat + d, n_lat)
+
+    for h, p in peers:
+        signal_to(barrier, zonal_peer(h, p)[1])
+    for d in range(1, n_lat):
+        signal_to(barrier, {"lat": lat_peer(d)})
+
+    def piece(h, p):
+        level = pl.multiple_of(lax.rem(hemisphere + h, 2) * half, half)
+        return waves.at[pl.ds(level, half), lax.rem(lon + p, n_lon)]
+
+    own = pltpu.make_async_copy(piece(0, 0), gathered.at[0, 0], local_sems.at[1])
+    own.start()
+    pl.semaphore_wait(barrier, len(peers) + n_lat - 1)
+
+    copies = []
+    for h, p in peers:
+        copy = remote(
+            piece(h, p),
+            gathered.at[h, p],
+            zonal_sends.at[h, p],
+            zonal_receives.at[h, p],
+            zonal_peer(h, p)[1],
+        )
+        copy.start()
+        copies.append(copy)
+
+    load.wait()
+
+    def split(s, carry):
+        full = matrix[s]
+        top = full.astype(jnp.bfloat16)
+        matrix_top[s] = top
+        matrix_rest[s] = (full - top.astype(jnp.float32)).astype(jnp.bfloat16)
+        return carry
+
+    lax.fori_loop(0, slots, split, 0)
+
+    own.wait()
+    for copy in copies:
+        copy.wait()
+
+    same = gathered[0, 0]
+    other = gathered[1, 0]
+    for p in range(1, n_lon):
+        same = same + gathered[0, p]
+        other = other + gathered[1, p]
+    sign = jnp.where(jnp.full(same.shape, hemisphere, jnp.int32) == 0, 1.0, -1.0)
+    for e, value in enumerate((same + other, (same - other) * sign)):
+        for w in range(width):
+            for level in range(half):
+                at = (2 * e + w % 2) * half + level
+                left[w // 2, at : at + 1, :] = value[level, w : w + 1, :]
+
+    degree = lax.broadcasted_iota(jnp.int32, (2 * half, degrees), 1)
+
+    def product(slot):
+        full = left[slot]
+        top = full.astype(jnp.bfloat16)
+        rest = (full - top.astype(jnp.float32)).astype(jnp.bfloat16)
+        result = jnp.dot(top, matrix_top[slot], preferred_element_type=jnp.float32)
+        result = result + jnp.dot(rest, matrix_top[slot], preferred_element_type=jnp.float32)
+        result = result + jnp.dot(top, matrix_rest[slot], preferred_element_type=jnp.float32)
+        wave = wave_map[lon * slots + slot]
+        even = ((degree + wave) & 1) == 0
+        chosen = jnp.where(even, result[: 2 * half], result[2 * half :])
+        return jnp.where(degree >= wave, chosen, 0.0)
+
+    sends = []
+    for d in range(n_lat - 1, 0, -1):
+        place = lat_peer(d)
+        for e in range(per_lat):
+            outgoing[d - 1, e] = product(place * per_lat + e)
+        copy = remote(
+            outgoing.at[d - 1],
+            partial.at[d - 1],
+            lat_sends.at[d - 1],
+            lat_receives.at[d - 1],
+            {"lat": place},
+        )
+        copy.start()
+        sends.append(copy)
+    mine = [product(lat * per_lat + e) for e in range(per_lat)]
+
+    scale = degree.astype(jnp.float32)
+    scale = scale * (scale + 1.0)
+    row = lax.broadcasted_iota(jnp.int32, (2 * half, degrees), 0)
+    coefficient = jnp.zeros((2 * half, degrees), jnp.float32)
+    for level in range(half):
+        coefficient = jnp.where(lax.rem(row, half) == level, helm[level], coefficient)
+    damping = 1.0 + coefficient * scale
+
+    for copy in sends:
+        copy.wait()
+    for e in range(per_lat):
+        total = mine[e]
+        for d in range(n_lat - 1):
+            total = total + partial[d, e]
+        total = total / damping
+        out[e, :, 0:degrees] = total[:half]
+        out[e, :, degrees : 2 * degrees] = total[half:]
+
+
+def spectral_sums(waves, legendre, wave_map, helm):
+    levels, n_lon, width, rows = waves.shape
+    half = levels // 2
+    slots, _, degrees = legendre.shape
+    n_lat = lax.axis_size("lat")
+    per_lat = slots // n_lat
+    f32, bf16 = jnp.float32, jnp.bfloat16
+    any_space = pl.BlockSpec(memory_space=pl.ANY)
+    smem = pl.BlockSpec(memory_space=pltpu.SMEM)
+    moved = pltpu.VMEM((n_lat - 1, per_lat, 2 * half, degrees), f32)
+    return pl.pallas_call(
+        spectral_kernel,
+        in_specs=[any_space, any_space, smem, smem],
+        out_specs=pl.BlockSpec(memory_space=pltpu.VMEM),
+        out_shape=jax.ShapeDtypeStruct((per_lat, half, 2 * degrees), f32),
+        scratch_shapes=[
+            pltpu.VMEM(legendre.shape, f32),
+            pltpu.VMEM(legendre.shape, bf16),
+            pltpu.VMEM(legendre.shape, bf16),
+            pltpu.VMEM((2, n_lon, half, width, rows), f32),
+            pltpu.VMEM((width // 2, 4 * half, rows), f32),
+            moved,
+            moved,
+            pltpu.SemaphoreType.DMA((2,)),
+            pltpu.SemaphoreType.DMA((2, n_lon)),
+            pltpu.SemaphoreType.DMA((2, n_lon)),
+            pltpu.SemaphoreType.DMA((n_lat - 1,)),
+            pltpu.SemaphoreType.DMA((n_lat - 1,)),
+        ],
+        compiler_params=pltpu.CompilerParams(collective_id=1, has_side_effects=True),
+    )(waves, legendre, wave_map, helm)
 
 
 def local(field, row_shift, col_shift, row_frac, col_frac, wave_map, legendre, helm_coef):
     grid = field[0]
-    levels, rows, cols = grid.shape
-    half = levels // 2
-    n_lon, n_lat, n_fold = (lax.axis_size(a) for a in ("lon", "lat", "fold"))
-    lon_place = lax.axis_index("lon")
-    table = zonal_table(wave_map, lon_place * cols, cols, cols * n_lon)
-    halos = halos_of(grid)
-    waves_here = interpolated_waves(
+    n_lon = lax.axis_size("lon")
+    *halos, table = exchanged_halos(grid, wave_map, grid.shape[2] * n_lon)
+    waves = interpolated_waves(
         grid,
         halos,
         (row_shift[0], col_shift[0]),
@@ -300,30 +650,8 @@
         table,
         n_lon,
     )
-    slots_here = wave_map.shape[0] // n_lon
-    hemisphere = lax.axis_index("fold") % 2
-    sign = (1 - 2 * hemisphere).astype(jnp.float32)
-    coeffs = scatter_sum(jnp.swapaxes(waves_here, 0, 1), "lon")
-    outgoing = lax.dynamic_slice_in_dim(coeffs, (1 - hemisphere) * half, half, 0)
-    incoming = lax.ppermute(outgoing, "fold", [(f, f ^ 1) for f in range(n_fold)])
-    kept = lax.dynamic_slice_in_dim(coeffs, hemisphere * half, half, 0)
-    folded = jnp.stack([kept + incoming, sign * (kept - incoming)], axis=0)
-    folded = jnp.transpose(folded.reshape(2, half, slots_here, 2, rows), (2, 3, 0, 1, 4))
-    degree_count = legendre.shape[2]
-    degrees = lax.iota(jnp.int32, degree_count)
-    waves = lax.dynamic_slice_in_dim(wave_map, lon_place * slots_here, slots_here)
-    product = jnp.einsum("sqelk,skn->selqn", folded, legendre, precision=lax.Precision.HIGHEST)
-    parity = (waves[:, None] + degrees[None, :]) % 2 == 0
-    keep = degrees[None, :] >= waves[:, None]
-    picked = jnp.where(parity[:, None, None, :], product[:, 0], product[:, 1])
-    picked = jnp.where(keep[:, None, None, :], picked, 0.0)
-    summed = scatter_sum(
-        picked.reshape(n_lat, slots_here // n_lat, half, 2 * degree_count), "lat"
-    )
-    degree_float = degrees.astype(jnp.float32)
-    pair = jnp.concatenate([degree_float, degree_float])
-    damping = 1.0 + helm_coef[None, :, None] * (pair * (pair + 1.0))[None, None, :]
-    return jnp.transpose(summed / damping, (1, 0, 2))[:, None, :, :]
+    result = spectral_sums(waves, legendre, wave_map, helm_coef)
+    return jnp.transpose(result, (1, 0, 2))[:, None, :, :]
 
 
 def solution(mesh):

time: 173 us -> 101 us (0.58)
  local copies, waits for them, and re-layouts: 63.3 us -> 1.57 us
  Pallas kernels: 62.7 us -> 98.1 us
  starting transfers between devices: 20.9 us -> 0 us
  other arithmetic: 11.6 us -> 0 us
  waiting for transfers between devices: 9.51 us -> 0 us
  matrix products: 1.92 us -> 0 us
    pallas_call x0 -> x2, Pallas kernels: none -> 35.4 us  [the longest x1 21.3 us: spectral_sums(): pl.pallas_call(spectral_kernel, in_specs=[any_space, any_space, smem, sme...]
    slice x17 -> x0, local copies, waits for them, and re-layouts: 26.9 us -> none  [the longest x3 7.72 us: edge(): grid[:, :, a:b]]
    ppermute x12 -> x0, starting transfers between devices: 20.9 us -> none  [the longest x6 7.81 us: scatter_sum(): lax.ppermute(piece, axis, [(i, (i + step) % count) for i in range(count)])]
    reshape x6 -> x0, local copies, waits for them, and re-layouts: 14.3 us -> none  [the longest x4 8.5 us: lanes_of(): jnp.transpose(pieces, (0, 1, 3, 2, 4)).reshape(front, groups, SUBS, LANES)]
    ppermute x12 -> x0, waiting for transfers between devices: 9.51 us -> none  [the longest x6 6.8 us: scatter_sum(): lax.ppermute(piece, axis, [(i, (i + step) % count) for i in range(count)])]
    transpose x2 -> x0, local copies, waits for them, and re-layouts: 5.15 us -> none  [lanes_of(): jnp.transpose(pieces, (0, 1, 3, 2, 4)).reshape(front, groups, SUBS, LANES)]
    squeeze x4 -> x0, local copies, waits for them, and re-layouts: 4.95 us -> none  [the longest x2 3.05 us: local(): picked = jnp.where(parity[:, None, None, :], product[:, 0], product[:, 1])]
    pad x2 -> x0, local copies, waits for them, and re-layouts: 4.38 us -> none  [lanes_of(): jnp.pad(pieces, ((0, 0), (0, groups * SLOTS - number), (0, 0), (0, 0)))]
  transfers between devices with their start and end apart: 12 -> 0, of which waited for: 7 -> 0; matrix products, arithmetic and copies ran while one was open for 15% -> 0% of each run, Pallas kernels for 0% -> 0%
where the time goes in v2:
time: 101 us; the launch traced here: 99.7 us
  Pallas kernels  98.1 us (97%)
  local copies, waits for them, and re-layouts  1.57 us (2%)
    pallas_call x1, Pallas kernels, interpolated_waves(): pl.pallas_call(interp_kernel, grid=(levels + 1,), in_specs=[ahead(x) for...  62.7 us
    pallas_call x1, Pallas kernels, spectral_sums(): pl.pallas_call(spectral_kernel, in_specs=[any_space, any_space, smem, sme...  21.3 us
    pallas_call x1, Pallas kernels, exchanged_halos(): pl.pallas_call(functools.partial(halo_kernel, lon_total), in_specs=[pl.Bl...  14.1 us

profile of v2, /device:TPU:1, one launch (start us, length us, event | category | flops | bytes accessed | tf_op | source)
XLA Modules:
  0.0 99.7 jit_solution(2713949795854405699)
XLA Ops:
  0.0 14.1 %shard_map.82 = (f32[12,8,640]{2,1,0:T(8,128)}, f32[12,8,640]{2,1,0:T(8,128)}, f32[12,2,8,128]{3,2,1,0:T(8,128)}, f32[12,2,8,128]{3,2,1,0:T(8,128)}, f32[2,1,8,1...) custom-call(f32[12,160,640]{2,1,0:T(8,128)} %bitcast.6, s32[16]{0:T(128)} %wave_map.3), custom_call_target="tpu_custom_call" | custom-call | tf_op jit(solution)/shard_map/pallas_call | solution.py:442
  14.2 62.7 %shard_map.83.waves = f32[12,4,8,160]{3,2,1,0:T(8,128)} custom-call(f32[12,160,640]{2,1,0:T(8,128)} %bitcast.7, f32[12,8,640]{2,1,0:T(8,128)} %get-tuple-element.12.north, f32[12,8,640]{2,1,0:T(8,128)} %get-tuple-element.13.south, f32[12,2,8,128]{3,2,1,0:T(8,128)} %get-tuple-element.14.west, f32[12,2,8,128]{3,2,1,0:T(8,128)} %get-tuple-element.15.east, ...), custom_call_target="tpu_custom_call" | custom-call | tf_op jit(solution)/shard_map/pallas_call | solution.py:210
  76.9 21.3 %shard_map.84 = f32[1,6,2560]{2,1,0:T(8,128)} custom-call(f32[12,4,8,160]{3,2,1,0:T(8,128)} %shard_map.83.waves, f32[4,160,1280]{2,1,0:T(8,128)} %legendre.1, s32[16]{0:T(128)} %wave_map.3, f32[6]{0:T(128)} %helm.1), custom_call_target="tpu_custom_call" | custom-call | tf_op jit(solution)/shard_map/pallas_call | solution.py:618
  98.2 1.6 %copy.9 = f32[6,1,1,2560]{3,2,1,0:T(1,128)} copy(f32[6,1,1,2560]{3,0,2,1:T(8,128)} %bitcast.12) | data formatting | bytes 122880 | tf_op jit(solution)/shard_map/broadcast_in_dim;transpose | solution.py:654
